TPU v7x, 8 devices: a whole 2x2x1 slice. The times are simulated.
8 devices in a mesh: dp: 1 (over z), tp: 8 (over y, x, core).
Axes of the slice: x: 2, y: 2, z: 1, core: 2. Of those that a mesh axis runs over, the one named last changes fastest.
Arguments:
- hidden: bfloat16 [4096, 1280], P(('dp', 'tp'))
- ln_gamma: float32 [1280], replicated
- ln_beta: float32 [1280], replicated
- out_embed: bfloat16 [51200, 1280], P('tp')
- vocab_valid: int32 [51200], P('tp')
- targets: int32 [4096], P(('dp', 'tp'))
- loss_mask: int32 [4096], P(('dp', 'tp'))
Outputs:
- output 1: float32 [4096], P(('dp', 'tp'))
- output 2: float32 [1], P('dp')
- output 3: bfloat16 [4096, 1280], P(('dp', 'tp'))
- output 4: float32 [51200, 1280], P(('dp', 'tp'))
- output 5: float32 [1280], P('dp')
- output 6: float32 [1280], P('dp')
All inputs are finite; a program needn't handle non-finite values.
Results may differ from a plain program's by a relative error of at most 0.001.
Values are sent between devices in bfloat16 or wider.
A program may use at most 1 GiB of HBM per device.

v0:
```python
import jax
import jax.numpy as jnp
from jax import lax
from jax.sharding import PartitionSpec as P

LN_EPS = 1e-5


def layer_norm(hidden32, ln_gamma, ln_beta):
    row_mean = jnp.mean(hidden32, axis=-1, keepdims=True)
    centered = hidden32 - row_mean
    row_var = jnp.mean(centered * centered, axis=-1, keepdims=True)
    return centered * lax.rsqrt(row_var + LN_EPS) * ln_gamma + ln_beta


def solution(mesh):
    tok_spec = P(("dp", "tp"))
    row_spec = P(("dp", "tp"), None)

    def local_step(hidden_blk, ln_gamma, ln_beta, embed_blk, valid_blk, tgt_blk, mask_blk):
        tok_local = hidden_blk.shape[0]
        shard_vocab = embed_blk.shape[0]
        shard_idx = lax.axis_index("tp")
        normed, ln_vjp = jax.vjp(layer_norm, hidden_blk.astype(jnp.float32), ln_gamma, ln_beta)
        x_all = lax.all_gather(normed.astype(jnp.bfloat16), "tp", axis=0, tiled=True)
        labels = lax.all_gather(jnp.stack([tgt_blk, mask_blk]), "tp", axis=1, tiled=True)
        weight = labels[1].astype(jnp.float32)
        logits = lax.dot_general(x_all, embed_blk, (((1,), (1,)), ((), ())), preferred_element_type=jnp.float32)
        allowed = (valid_blk > 0)[None, :]
        local_max = jnp.max(jnp.where(allowed, logits, -jnp.inf), axis=1)
        row_max = lax.pmax(local_max, "tp")
        shifted_exp = jnp.where(allowed, jnp.exp(logits - row_max[:, None]), 0.0)
        target_hit = (jnp.arange(shard_vocab) + shard_idx * shard_vocab)[None, :] == labels[0][:, None]
        picked_part = jnp.sum(jnp.where(target_hit, logits, 0.0), axis=1)
        tok_stats = lax.psum(jnp.stack([jnp.sum(shifted_exp, axis=1), picked_part]), "tp")
        log_norm = row_max + jnp.log(tok_stats[0])
        tok_count = jnp.sum(weight)
        tok_loss = (log_norm - tok_stats[1]) * weight
        mean_loss = (jnp.sum(tok_loss) / tok_count).reshape(1)
        soft_probs = shifted_exp / tok_stats[0][:, None]
        d_logits = ((soft_probs - target_hit.astype(jnp.float32)) * (weight / tok_count)[:, None]).astype(jnp.bfloat16)
        d_embed = lax.dot_general(d_logits, x_all, (((0,), (0,)), ((), ())), preferred_element_type=jnp.float32)
        dx_part = jnp.dot(d_logits, embed_blk, preferred_element_type=jnp.float32)
        dx_local = lax.psum_scatter(dx_part, "tp", scatter_dimension=0, tiled=True)
        d_hidden, d_gamma, d_beta = ln_vjp(dx_local)
        ln_grads = lax.psum(jnp.stack([d_gamma, d_beta]), "tp")
        loss_local = lax.dynamic_slice_in_dim(tok_loss, shard_idx * tok_local, tok_local)
        return loss_local, mean_loss, d_hidden.astype(jnp.bfloat16), d_embed, ln_grads[0], ln_grads[1]

    return jax.shard_map(local_step, mesh=mesh, in_specs=(row_spec, P(), P(), P("tp", None), P("tp"), tok_spec, tok_spec), out_specs=(tok_spec, P("dp"), row_spec, row_spec, P("dp"), P("dp")), check_vma=False)
```

profile of v0, /device:TPU:0, one launch (start us, length us, event | category | flops | bytes accessed | tf_op | source)
XLA Modules:
  0.0 542.6 jit_solution(14301054531334540501)
XLA Ops:
  7.2 0.0 all-gather.2.cloned.1.call-start
  7.2 1.6 convert_reduce_fusion
  8.8 0.0 copy-start.3
  8.8 1.8 fusion.14
  10.6 0.0 copy-start.7
  10.6 0.6 copy-done.7
  11.2 0.0 copy-done.3
  11.2 0.0 copy-start.5
  11.2 0.6 copy-done.5
  11.8 2.9 fusion.12
  14.7 0.0 all-gather.2.cloned.1.call-update
  14.7 0.0 reduce-scatter.2.cloned.1.call-start
  14.8 0.7 pad_add_fusion
  15.5 14.2 %all_gather.7 = s32[2,4096]{1,0:T(2,128)S(1)} all-gather(s32[2,512]{1,0:T(2,128)S(1)} %pad_add_fusion), channel_id=1, replica_groups=mesh['dp'=1,'tp'=8] {'tp'}, dimensions={1}, use_global_device_ids=true | all-gather | bytes 36864 | tf_op jit(solution)/shard_map/all_gather | solution.py:26
  29.8 0.6 fusion.17
  30.4 0.8 broadcast_compare_fusion
  31.1 0.6 fusion.21
  31.8 43.6 %all-gather.2.cloned.1.call-done = bf16[4096,1280]{1,0:T(8,128)(2,1)} async-done(((bf16[512,1280]{1,0:T(8,128)(2,1)}), bf16[4096,1280]{1,0:T(8,128)(2,1)}) %all-gather.2.cloned.1.call-update) | async-done | bytes 10485776 | tf_op jit(solution)/shard_map/all_gather | solution.py:25
  75.3 81.3 %select_reduce_fusion = (f32[4096]{0:T(1024)S(1)}, f32[4096,6400]{1,0:T(8,128)}) fusion(pred[6400]{0:T(1024)(128)(4,1)S(1)} %broadcast_compare_fusion, bf16[4096,1280]{1,0:T(8,128)(2,1)} %all-gather.2.cloned.1.call-done, bf16[6400,1280]{1,0:T(8,128)(2,1)} %param.10), kind=kOutput, calls=%fused_computation.7 | convolution fusion | flops 67161288704 | bytes 131750144 | tf_op jit(solution)/shard_map/dot_general | solution.py:28
  156.6 22.3 %pmax.7 = f32[4096]{0:T(1024)S(1)} all-reduce(f32[4096]{0:T(1024)S(1)} %get-tuple-element.22), channel_id=1, replica_groups=mesh['dp'=1,'tp'=8] {'tp'}, use_global_device_ids=true, to_apply=%region_3.4 | all-reduce | flops 4096 | bytes 32768 | tf_op jit(solution)/shard_map/pmax | solution.py:31
  178.9 0.0 copy-start.2
  178.9 39.4 %fusion.4 = (f32[4096]{0:T(1024)S(1)}, f32[4096]{0:T(1024)S(1)}) fusion(f32[4096,6400]{1,0:T(8,128)} %get-tuple-element.23, f32[4096]{0:T(1024)S(1)} %pmax.7, pred[6400]{0:T(1024)(128)(4,1)S(1)} %broadcast_compare_fusion, s32[4096]{0:T(1024)S(1)} %bitcast.15, s32[6400]{0:T(1024)S(1)} %iota_add_fusion), kind=kLoop, calls=%fused_computation.8 | loop fusion | flops 157278208 | bytes 104955136 | tf_op jit(solution)/shard_map/reduce_sum | solution.py:35
  218.3 24.3 %psum.14 = f32[2,4096]{1,0:T(2,128)S(1)} all-reduce(f32[2,4096]{1,0:T(2,128)S(1)} %pad_maximum_fusion), channel_id=1, replica_groups=mesh['dp'=1,'tp'=8] {'tp'}, use_global_device_ids=true, to_apply=%region_6.7 | all-reduce | flops 8192 | bytes 65536 | tf_op jit(solution)/shard_map/psum | solution.py:35
  242.7 0.0 copy-done.2
  242.7 1.9 fusion.19
  244.5 51.6 %fusion.3 = bf16[4096,6400]{1,0:T(8,128)(2,1)} fusion(f32[4096,6400]{1,0:T(8,128)} %get-tuple-element.23, f32[4096]{0:T(1024)S(1)} %get-tuple-element.21, f32[4096]{0:T(1024)S(1)} %bitcast.18, s32[6400]{0:T(1024)S(1)} %iota_add_fusion, f32[4096]{0:T(1024)S(1)} %pmax.7, s32[4096]{0:T(1024)S(1)} %bitcast.16, pred[6400]{0:T(1024)(128)(4,1)S(1)} %broadcast_compare_fusion), kind=kLoop, calls=%fused_computation.5 | loop fusion | flops 209715200 | bytes 157383936 | tf_op jit(solution)/shard_map/convert_element_type | solution.py:41
  296.1 77.9 %fusion.22 = f32[4096,1280]{1,0:T(8,128)} fusion(bf16[4096,6400]{1,0:T(8,128)(2,1)} %fusion.3, bf16[6400,1280]{1,0:T(8,128)(2,1)} %param.10), kind=kOutput, calls=%fused_computation.44 | convolution fusion | flops 67108864000 | bytes 89784320 | tf_op jit(solution)/shard_map/dot_general | solution.py:43
  374.0 0.0 reduce-scatter.2.cloned.1.call-update
  375.4 1.3 dynamic_slice.3
  376.7 0.0 copy-start
  376.7 0.0 copy-start.1
  376.7 0.0 copy-start.4
  376.7 0.0 copy-start.6
  376.7 0.0 copy-start.8
  376.7 80.5 %fusion.23 = f32[6400,1280]{1,0:T(8,128)} fusion(bf16[4096,6400]{1,0:T(8,128)(2,1)} %fusion.3, bf16[4096,1280]{1,0:T(8,128)(2,1)} %all-gather.2.cloned.1.call-done), kind=kOutput, calls=%fused_computation.45 | convolution fusion | flops 67108864000 | bytes 95682560 | tf_op jit(solution)/shard_map/dot_general | solution.py:42
  457.2 44.7 %reduce-scatter.2.cloned.1.call-done = f32[512,1280]{1,0:T(8,128)} async-done(((f32[4096,1280]{1,0:T(8,128)}), f32[512,1280]{1,0:T(8,128)}) %reduce-scatter.2.cloned.1.call-update) | async-done | bytes 2621456 | tf_op jit(solution)/shard_map/reduce_scatter | solution.py:44
  501.9 0.0 copy-done
  501.9 0.0 copy-done.1
  501.9 0.0 copy-done.4
  501.9 0.0 copy-done.6
  501.9 2.7 fusion.13
  504.5 0.0 copy-done.8
  504.5 4.0 fusion.18
  508.6 22.4 %psum.15 = f32[2,1280]{1,0:T(2,128)S(1)} all-reduce(f32[2,1280]{1,0:T(2,128)S(1)} %pad_maximum_fusion.1), channel_id=1, replica_groups=mesh['dp'=1,'tp'=8] {'tp'}, use_global_device_ids=true, to_apply=%region_14.15 | all-reduce | flops 2560 | bytes 20480 | tf_op jit(solution)/shard_map/psum | solution.py:46
  531.0 0.6 slice_reduce_fusion
  531.6 3.0 add_convert_fusion
  (10 shorter events, 0.1 us)
Async XLA Ops:
  7.2 68.2 %all-gather.2.cloned.1.call-start = ((), (), s32[]{:S(2)}) async-start(), calls=%async_computation.1 | async-start | bytes 11796480 | tf_op jit(solution)/shard_map/all_gather | solution.py:25
  8.8 2.4 copy-start.3
  10.6 0.6 copy-start.7
  11.2 0.6 copy-start.5
  14.7 487.1 %reduce-scatter.2.cloned.1.call-start = ((), (), s32[]{:S(2)}) async-start(), calls=%async_computation.2 | async-start | bytes 23592960 | tf_op jit(solution)/shard_map/reduce_scatter | solution.py:44
  178.9 63.8 %copy-start.2 = (f32[1,4096]{1,0:T(1,128)S(1)}, f32[1,4096]{1,0:T(1,128)}, u32[]{:S(2)}) copy-start(f32[1,4096]{1,0:T(1,128)} %get-tuple-element.20) | copy-start | bytes 49156
  376.7 125.2 %copy-start = (bf16[512,1280]{1,0:T(8,128)(2,1)S(1)}, bf16[512,1280]{1,0:T(8,128)(2,1)}, u32[]{:S(2)}) copy-start(bf16[512,1280]{1,0:T(8,128)(2,1)} %param.7) | copy-start | bytes 3932164
  376.7 125.2 %copy-start.1 = (f32[1280]{0:T(1024)S(1)}, f32[1280]{0:T(1024)}, u32[]{:S(2)}) copy-start(f32[1280]{0:T(1024)} %param.8) | copy-start | bytes 15364
  376.7 125.2 %copy-start.4 = (f32[512]{0:T(512)S(1)}, f32[512]{0:T(512)}, u32[]{:S(2)}) copy-start(f32[512]{0:T(512)} %copy-done.3) | copy-start | bytes 6148
  376.7 125.2 %copy-start.6 = (f32[512]{0:T(512)S(1)}, f32[512]{0:T(512)}, u32[]{:S(2)}) copy-start(f32[512]{0:T(512)} %copy-done.5) | copy-start | bytes 6148
  376.7 127.8 %copy-start.8 = (f32[512]{0:T(512)S(1)}, f32[512]{0:T(512)}, u32[]{:S(2)}) copy-start(f32[512]{0:T(512)} %copy-done.7) | copy-start | bytes 6148
Sparse Core Ops, SparseCore 0:
  14.9 60.4 all-gather.1
  374.1 127.6 reduce-scatter.1
where the time goes:
time: 543 us
  matrix products  240 us (44%)
  other arithmetic  112 us (21%)
  waiting for transfers between devices  88.3 us (16%)
  blocking collectives  83.2 us (15%)
  between operations  16.6 us (3%)
    dot_general x1, matrix products, local_step(): lax.dot_general(x_all, embed_blk, (((1,), (1,)), ((), ())), preferred_ele...  81.3 us
    dot_general x1, matrix products, local_step(): lax.dot_general(d_logits, x_all, (((0,), (0,)), ((), ())), preferred_elem...  80.5 us
    dot_general x1, matrix products, local_step(): dx_part = jnp.dot(d_logits, embed_blk, preferred_element_type=jnp.float32)  77.9 us
    convert_element_type x1, other arithmetic, local_step(): ((soft_probs - target_hit.astype(jnp.float32)) * (weight / tok_count)[:,...  51.6 us
    reduce_scatter x1, waiting for transfers between devices, local_step(): dx_local = lax.psum_scatter(dx_part, 'tp', scatter_dimension=0, tiled=True)  44.7 us
    all_gather x1, waiting for transfers between devices, local_step(): lax.all_gather(normed.astype(jnp.bfloat16), 'tp', axis=0, tiled=True)  43.6 us
    reduce_sum x1, other arithmetic, local_step(): jnp.sum(shifted_exp, axis=1)  39.4 us
    psum x1, blocking collectives, local_step(): lax.psum(jnp.stack([jnp.sum(shifted_exp, axis=1), picked_part]), 'tp')  24.3 us
  transfers between devices with their start and end apart: 2, of which 2 were waited for; matrix products, arithmetic and copies ran while one was open for 16% of the time, Pallas kernels for 0%

commit v1 on v0

v1 whole, which is shorter than its diff:
```python
import functools

import jax
import jax.numpy as jnp
from jax import lax
from jax.experimental import pallas as pl
from jax.experimental.pallas import tpu as pltpu
from jax.sharding import PartitionSpec as P

LN_EPS = 1e-5
LANES = 128
NB = 5
LAG = NB + 1
LOW = float(jnp.finfo(jnp.float32).min)
MESH = pl.DeviceIdType.MESH
NT = (((1,), (1,)), ((), ()))


def _spread(row):
    return jnp.broadcast_to(row, (LANES, LANES)).T


def fused_kernel(
    hid_ref, gam_ref, bet_ref, emb_hbm, valid_ref, tm_ref,
    dz_hbm, xall_hbm, dh_ref, loss_ref, gb_ref,
    xv, ev, ring, acc, dzb, bias, m_sc, s_sc, p_sc, t1_sc, t2_sc, lse_sc, w_sc,
    tm_all, st_send, st_recv, r0, r1, r2, gb_send, gb_recv,
    e_sem, ag_send, ag_recv, fw_send, tm_send, tm_recv, st_ssem, st_rsem,
    s0, q0, s1, q1, s2, q2, free0, free1, free2, gb_ssem, gb_rsem, dz_sem, x_sem,
):
    nc, tok, dim = xv.shape
    vb = ev.shape[1]
    own = tok // 8
    half = tok // 2
    me = lax.axis_index("tp")
    core = lax.rem(me, 2)
    xc = lax.rem(me // 2, 2)
    yc = me // 4

    def dev(y, x, k):
        return y * 4 + x * 2 + k

    def slot_of(y, x, k):
        return k * 4 + y * 2 + x

    sib = dev(yc, xc, 1 - core)
    xn = dev(yc, 1 - xc, core)
    yn = dev(1 - yc, xc, core)
    dn = dev(1 - yc, 1 - xc, core)
    remote = ((xn, slot_of(yc, 1 - xc, core)), (yn, slot_of(1 - yc, xc, core)), (dn, slot_of(1 - yc, 1 - xc, core)))
    my_slot = slot_of(yc, xc, core)
    first_n = jnp.where(core == 0, xn, yn)
    second_n = jnp.where(core == 0, yn, xn)

    def rcopy(src, dst, ssem, rsem, to):
        return pltpu.make_async_remote_copy(src_ref=src, dst_ref=dst, send_sem=ssem, recv_sem=rsem, device_id={"tp": to}, device_id_type=MESH)

    def rows(slot):
        return pl.ds(pl.multiple_of(slot * own, own), own)

    for j in range(NB):
        pltpu.make_async_copy(emb_hbm.at[j], ev.at[j], e_sem.at[j]).start()

    barrier = pltpu.get_barrier_semaphore()
    for k in range(1, 8):
        pl.semaphore_signal(barrier, inc=1, device_id={"tp": lax.rem(me + k, 8)}, device_id_type=MESH)
    pl.semaphore_wait(barrier, 7)

    tm_all[me] = tm_ref[...]

    def tm_copy(k):
        return rcopy(tm_ref, tm_all.at[me], tm_send.at[k], tm_recv.at[k], lax.rem(me + k, 8))

    for k in range(1, 8):
        tm_copy(k).start()

    def ln(c):
        h = hid_ref[pl.ds(pl.multiple_of(c * own, own), own), :].astype(jnp.float32)
        cen = h - jnp.mean(h, axis=1, keepdims=True)
        rstd = lax.rsqrt(jnp.mean(cen * cen, axis=1, keepdims=True) + LN_EPS)
        return cen * rstd, rstd

    def ag_copy(c, k):
        r = xv.at[c, rows(my_slot)]
        return rcopy(r, r, ag_send.at[c, k], ag_recv.at[c, k], (xn, yn, dn, sib)[k])

    def fw_copy(c, k):
        r = xv.at[c, rows(remote[k][1])]
        return rcopy(r, r, fw_send.at[c, k], ag_recv.at[c, 4 + k], sib)

    def ln_body(c, _):
        xhat, _r = ln(c)
        xv[c, rows(my_slot), :] = (xhat * gam_ref[...] + bet_ref[...]).astype(jnp.bfloat16)

        @pl.when(c >= 1)
        def _():
            for k in (2, 0, 1, 3):
                ag_copy(c - 1, k).start()
        return 0

    lax.fori_loop(0, nc, ln_body, 0)
    for k in (2, 0, 1, 3):
        ag_copy(nc - 1, k).start()

    bias[...] = jnp.where(valid_ref[...] > 0, 0.0, -jnp.inf)
    gb_send[...] = jnp.zeros_like(gb_send)

    def recv_remote(c):
        for k in range(3):
            ag_copy(c, k).wait_recv()

    def forward(c):
        recv_remote(c)
        for k in range(3):
            fw_copy(c, k).start()

    for k in range(1, 8):
        tm_copy(k).wait_recv()
    count = jnp.zeros((8, LANES), jnp.float32)
    for d in range(8):
        count = count + tm_all[d, 1]
    count = jnp.sum(jnp.sum(count, axis=1, keepdims=True), axis=0, keepdims=True)
    inv_n = 1.0 / count

    def tm_rows(c, which):
        out = []
        for q in range(4):
            k, y = q // 2, q % 2
            out.append(tm_all[dev(y, 0, k), which, pl.ds(c, 1), :] + tm_all[dev(y, 1, k), which, pl.ds(c, 1), :])
        return out

    forward(0)
    lane = lax.broadcasted_iota(jnp.int32, (tok, LANES), 1)

    def st_copy(c, k):
        return rcopy(st_send.at[c], st_recv.at[c, me], st_ssem.at[c, k], st_rsem.at[c, k], lax.rem(me + k, 8))

    def send_stats(c):
        li = lax.broadcasted_iota(jnp.int32, (LANES, LANES), 1)
        for q in range(4):
            r = pl.ds(q * LANES, LANES)
            m = m_sc[r]
            mx = jnp.max(m, axis=1, keepdims=True)
            s = jnp.sum(s_sc[r] * jnp.exp(m - mx), axis=1, keepdims=True)
            p = jnp.sum(p_sc[r], axis=1, keepdims=True)
            v = jnp.where(li == 0, mx, jnp.where(li == 1, s, p))
            st_send[c, q] = v.T[:8]
        st_recv[c, me] = st_send[c]
        for k in range(1, 8):
            st_copy(c, k).start()

    def use_stats(c):
        for k in range(1, 8):
            st_copy(c, k).wait_recv()
        tg = tm_rows(c, 0)
        mk = tm_rows(c, 1)
        for q in range(4):
            mx = st_recv[c, 0, q, 0:1]
            for d in range(1, 8):
                mx = jnp.maximum(mx, st_recv[c, d, q, 0:1])
            s = jnp.zeros_like(mx)
            p = jnp.zeros_like(mx)
            for d in range(8):
                s = s + st_recv[c, d, q, 1:2] * jnp.exp(st_recv[c, d, q, 0:1] - mx)
                p = p + st_recv[c, d, q, 2:3]
            lse = mx + jnp.log(s)
            loss_ref[c, pl.ds(q, 1), :] = (lse - p) * mk[q]
            r = pl.ds(q * LANES, LANES)
            lse_sc[r] = _spread(lse)
            w_sc[r] = _spread(mk[q] * inv_n)
            t2_sc[r] = _spread(tg[q]).astype(jnp.int32)

    def begin_chunk(c):
        for k in range(3, 7):
            if k == 3:
                ag_copy(c, 3).wait_recv()
            else:
                fw_copy(c, k - 4).wait_recv()
        pltpu.make_async_copy(xv.at[c], xall_hbm.at[c], x_sem.at[c]).start()
        m_sc[...] = jnp.full(m_sc.shape, LOW, jnp.float32)
        s_sc[...] = jnp.zeros_like(s_sc)
        p_sc[...] = jnp.zeros_like(p_sc)
        tg = tm_rows(c, 0)
        for q in range(4):
            t1_sc[pl.ds(q * LANES, LANES)] = _spread(tg[q]).astype(jnp.int32)

    def first_src(b):
        return jnp.where(core == 0, b * 2 + (1 - xc), (1 - yc) * 2 + b)

    def first_keep(b):
        return jnp.where(core == 0, b * 2 + xc, yc * 2 + b)

    own2 = jnp.where(core == 0, yc, xc)

    def c0(c):
        a = lax.rem(c, 2)
        return rcopy(acc.at[a, pl.ds(pl.multiple_of((1 - core) * half, half), half)], r0.at[a], s0.at[a], q0.at[a], sib)

    def c1(c, b):
        a = lax.rem(c, 2)
        return rcopy(r0.at[a, rows(first_src(b))], r1.at[a, b], s1.at[a, b], q1.at[a, b], first_n)

    def c2(c):
        a = lax.rem(c, 2)
        return rcopy(r1.at[a, 1 - own2], r2.at[a], s2.at[a], q2.at[a], second_n)

    def stage0(c):
        @pl.when(c >= 2)
        def _():
            pl.semaphore_wait(free0, 1)
        c0(c).start()

    def stage1(c):
        a = lax.rem(c, 2)
        c0(c).wait()
        r0[a] = r0[a] + acc[a, pl.ds(pl.multiple_of(core * half, half), half)]

        @pl.when(c >= 2)
        def _():
            pl.semaphore_wait(free1, 1)
        for b in range(2):
            c1(c, b).start()

    def stage2(c):
        a = lax.rem(c, 2)
        for b in range(2):
            c1(c, b).wait()
        for b in range(2):
            r1[a, b] = r1[a, b] + r0[a, rows(first_keep(b))]

        @pl.when(c >= 2)
        def _():
            pl.semaphore_wait(free2, 1)
        c2(c).start()

        @pl.when(c < nc - 2)
        def _():
            pl.semaphore_signal(free0, inc=1, device_id={"tp": sib}, device_id_type=MESH)

    def stage3(c):
        a = lax.rem(c, 2)
        c2(c).wait()
        dy = r1[a, own2] + r2[a]

        @pl.when(c < nc - 2)
        def _():
            pl.semaphore_signal(free1, inc=1, device_id={"tp": first_n}, device_id_type=MESH)
            pl.semaphore_signal(free2, inc=1, device_id={"tp": second_n}, device_id_type=MESH)
        xhat, rstd = ln(c)
        gb_send[0:1] += jnp.sum(dy * xhat, axis=0, keepdims=True)
        gb_send[1:2] += jnp.sum(dy, axis=0, keepdims=True)
        dxh = dy * gam_ref[...]
        m1 = jnp.mean(dxh, axis=1, keepdims=True)
        m2 = jnp.mean(dxh * xhat, axis=1, keepdims=True)
        dh_ref[pl.ds(pl.multiple_of(c * own, own), own), :] = (rstd * (dxh - m1 - xhat * m2)).astype(jnp.bfloat16)

    base = me * (NB * vb)

    def dz_copy(t):
        a = lax.rem(t, 2)
        t2 = t - LAG
        return pltpu.make_async_copy(dzb.at[a], dz_hbm.at[lax.rem(t2, NB), pl.ds(pl.multiple_of((t2 // NB) * tok, tok), tok)], dz_sem.at[a])

    def compute(t, do1, do2):
        slot = lax.rem(t, LAG)
        a2 = lax.rem(t, 2)
        if do2:
            t2 = t - LAG
            j2 = lax.rem(t2, NB)
            tr = t2_sc[...] - (base + j2 * vb)
            for k in range(vb // LANES):
                col = k * LANES
                p = jnp.exp(ring[slot, :, pl.ds(col, LANES)] - lse_sc[...])
                p = jnp.where(tr == lane + col, p - 1.0, p) * w_sc[...]
                dzb[a2, :, pl.ds(col, LANES)] = p.astype(jnp.bfloat16)
        if do1:
            j1 = lax.rem(t, NB)
            tr = t1_sc[...] - (base + j1 * vb)
            z = lax.dot_general(xv[t // NB], ev[j1], NT, preferred_element_type=jnp.float32) + bias[j1]
            ring[slot] = z
            zs = [z[:, k * LANES:(k + 1) * LANES] for k in range(vb // LANES)]
            m0 = m_sc[...]
            m = m0
            for q in zs:
                m = jnp.maximum(m, q)
            s = s_sc[...] * jnp.exp(m0 - m)
            pk = p_sc[...]
            for k, q in enumerate(zs):
                s = s + jnp.exp(q - m)
                pk = pk + jnp.where(tr == lane + k * LANES, q, 0.0)
            m_sc[...] = m
            s_sc[...] = s
            p_sc[...] = pk
        if do2:
            a = lax.rem(t2 // NB, 2)
            acc[a] = acc[a] + jnp.dot(dzb[a2], ev[j2], preferred_element_type=jnp.float32)

    def step(t, do1, do2):
        ph = lax.rem(t, NB)
        if do1:
            @pl.when(ph == 0)
            def _():
                begin_chunk(t // NB)

            @pl.when((ph == 2) & (t // NB + 1 < nc))
            def _():
                forward(t // NB + 1)

            @pl.when(t < NB)
            def _():
                pltpu.make_async_copy(emb_hbm.at[ph], ev.at[ph], e_sem.at[ph]).wait()
        if do2:
            @pl.when((ph == 1) & (t >= 11))
            def _():
                stage0((t - 11) // NB)

            @pl.when(ph == 1)
            def _():
                c = (t - LAG) // NB
                use_stats(c)
                acc[lax.rem(c, 2)] = jnp.zeros((tok, dim), jnp.float32)

            @pl.when((ph == 2) & (t >= 17))
            def _():
                stage3((t - 17) // NB)

            @pl.when((ph == 2) & (t >= 12))
            def _():
                stage1((t - 12) // NB)

            @pl.when((ph == 0) & (t >= 15))
            def _():
                stage2((t - 15) // NB)

            @pl.when(t >= LAG + 2)
            def _():
                dz_copy(t - 2).wait()
        compute(t, do1, do2)
        if do2:
            dz_copy(t).start()
        if do1:
            @pl.when(ph == NB - 1)
            def _():
                send_stats(t // NB)

    def loop(lo, hi, do1, do2):
        def body(t, _):
            step(t, do1, do2)
            return 0
        lax.fori_loop(lo, hi, body, 0)

    total = NB * nc
    loop(0, LAG, True, False)
    loop(LAG, total, True, True)
    loop(total, total + LAG, False, True)

    last = nc - 1
    stage0(last)
    stage3(last - 1)
    stage1(last)
    stage2(last)
    stage3(last)

    def gb_copy(k):
        return rcopy(gb_send, gb_recv.at[me], gb_ssem.at[k], gb_rsem.at[k], lax.rem(me + k, 8))

    for k in range(1, 8):
        gb_copy(k).start()
    gb_recv[me] = gb_send[...]
    for t in (total + LAG - 2, total + LAG - 1):
        dz_copy(t).wait()

    def drain(c, _):
        for k in range(4):
            ag_copy(c, k).wait_send()
        for k in range(3):
            fw_copy(c, k).wait_send()
        for k in range(1, 8):
            st_copy(c, k).wait_send()
        pltpu.make_async_copy(xv.at[c], xall_hbm.at[c], x_sem.at[c]).wait()
        return 0

    lax.fori_loop(0, nc, drain, 0)
    for k in range(1, 8):
        tm_copy(k).wait_send()
        gb_copy(k).wait()
    tot = gb_recv[0]
    for d in range(1, 8):
        tot = tot + gb_recv[d]
    gb_ref[...] = tot
    gb_ref[2:3] = jnp.broadcast_to(count, (1, dim))


def fused(hidden, gamma, beta, embed, valid, tm):
    tok, dim = hidden.shape
    nc = 8
    own = tok // nc
    vb = embed.shape[0] // NB
    full = own * 8
    f32, bf16 = jnp.float32, jnp.bfloat16
    sds = jax.ShapeDtypeStruct
    vmem = pl.BlockSpec(memory_space=pltpu.VMEM)
    hbm = pl.BlockSpec(memory_space=pl.ANY)
    col = pltpu.VMEM((full, LANES), f32)
    coli = pltpu.VMEM((full, LANES), jnp.int32)
    dma, reg = pltpu.SemaphoreType.DMA, pltpu.SemaphoreType.REGULAR
    flops = 4 * full * nc * embed.shape[0] * dim
    return pl.pallas_call(
        fused_kernel,
        out_shape=(
            sds((NB, nc * full, vb), bf16),
            sds((nc, full, dim), bf16),
            sds((tok, dim), bf16),
            sds((nc, 4, LANES), f32),
            sds((8, dim), f32),
        ),
        in_specs=[vmem, vmem, vmem, hbm, vmem, vmem],
        out_specs=(hbm, hbm, vmem, vmem, vmem),
        scratch_shapes=[
            pltpu.VMEM((nc, full, dim), bf16),
            pltpu.VMEM((NB, vb, dim), bf16),
            pltpu.VMEM((LAG, full, vb), f32),
            pltpu.VMEM((2, full, dim), f32),
            pltpu.VMEM((2, full, vb), bf16),
            pltpu.VMEM((NB, 1, vb), f32),
            col, col, col, coli, coli, col, col,
            pltpu.VMEM((8, 2, nc, LANES), f32),
            pltpu.VMEM((nc, 4, 8, LANES), f32),
            pltpu.VMEM((nc, 8, 4, 8, LANES), f32),
            pltpu.VMEM((2, full // 2, dim), f32),
            pltpu.VMEM((2, 2, own, dim), f32),
            pltpu.VMEM((2, own, dim), f32),
            pltpu.VMEM((8, dim), f32),
            pltpu.VMEM((8, 8, dim), f32),
            dma((NB,)), dma((nc, 4)), dma((nc, 7)), dma((nc, 3)), dma((8,)), dma((8,)), dma((nc, 8)), dma((nc, 8)),
            dma((2,)), dma((2,)), dma((2, 2)), dma((2, 2)), dma((2,)), dma((2,)),
            reg, reg, reg, dma((8,)), dma((8,)), dma((2,)), dma((nc,)),
        ],
        compiler_params=pltpu.CompilerParams(collective_id=0, has_side_effects=True, vmem_limit_bytes=67043328),
        cost_estimate=pl.CostEstimate(flops=flops, bytes_accessed=100_000_000, transcendentals=0),
    )(hidden, gamma, beta, embed.reshape(NB, vb, dim), valid, tm)


def grad_kernel(dz_ref, x_ref, o_ref):
    o_ref[...] = lax.dot_general(dz_ref[...], x_ref[...], (((0,), (0,)), ((), ())), preferred_element_type=jnp.float32)


def embed_grad(dz, x):
    nb, toks, vb = dz.shape
    dim = x.shape[1]
    mb = vb // 2
    return pl.pallas_call(
        grad_kernel,
        grid=(nb, 2),
        out_shape=jax.ShapeDtypeStruct((nb * vb, dim), jnp.float32),
        in_specs=[
            pl.BlockSpec((None, toks, mb), lambda i, k: (i, 0, k)),
            pl.BlockSpec((toks, dim), lambda i, k: (0, 0), pipeline_mode=pl.Buffered(1)),
        ],
        out_specs=pl.BlockSpec((mb, dim), lambda i, k: (i * 2 + k, 0)),
        compiler_params=pltpu.CompilerParams(vmem_limit_bytes=62 * 1024 * 1024),
        cost_estimate=pl.CostEstimate(flops=2 * toks * nb * vb * dim, bytes_accessed=100_000_000, transcendentals=0),
    )(dz, x)


def solution(mesh):
    tok_spec = P(("dp", "tp"))
    row_spec = P(("dp", "tp"), None)

    def local_step(hidden, gamma, beta, embed, valid, tgt, mask):
        tok, dim = hidden.shape
        own = tok // 8
        me = lax.axis_index("tp")
        core, xc, yc = me % 2, (me // 2) % 2, me // 4
        slot = core * 4 + yc * 2 + xc
        tm = jnp.stack([tgt, mask]).astype(jnp.float32).reshape(2, 8, 1, own)
        tm = jnp.where((jnp.arange(2) == xc)[None, None, :, None], tm, 0.0).reshape(2, 8, 2 * own)
        dz, x_all, d_hidden, loss, gb = fused(
            hidden, gamma.reshape(1, dim), beta.reshape(1, dim), embed, valid.reshape(NB, 1, -1), tm)
        d_embed = embed_grad(dz, x_all.reshape(-1, dim))
        tok_loss = lax.dynamic_index_in_dim(loss.reshape(8, 8, own), slot, axis=1, keepdims=False).reshape(-1)
        mean_loss = jnp.sum(loss) / gb[2, :1]
        return tok_loss, mean_loss, d_hidden, d_embed, gb[0], gb[1]

    return jax.shard_map(
        local_step,
        mesh=mesh,
        in_specs=(row_spec, P(), P(), P("tp", None), P("tp"), tok_spec, tok_spec),
        out_specs=(tok_spec, P("dp"), row_spec, row_spec, P("dp"), P("dp")),
        check_vma=False,
    )
```

time: 543 us -> 359 us (0.66)
  Pallas kernels: 0 us -> 342 us
  matrix products: 240 us -> 0 us
  other arithmetic: 112 us -> 1.95 us
  waiting for transfers between devices: 88.3 us -> 0 us
  blocking collectives: 83.2 us -> 0 us
  between operations: 16.6 us -> 3.18 us
  local copies, waits for them, and re-layouts: 3.2 us -> 10.9 us
    pallas_call x0 -> x2, Pallas kernels: none -> 342 us  [the longest x1 265 us: fused(): pl.pallas_call(fused_kernel, out_shape=(sds((NB, nc * full, vb), bf16), s...]
    dot_general x3 -> x0, matrix products: 240 us -> none  [the longest x1 81.3 us: local_step(): lax.dot_general(x_all, embed_blk, (((1,), (1,)), ((), ())), preferred_ele...]
    convert_element_type x3 -> x1, other arithmetic: 57.5 us -> 0.01 us  [local_step(): tm = jnp.stack([tgt, mask]).astype(jnp.float32).reshape(2, 8, 1, own)]
    reduce_sum x7 -> x1, other arithmetic: 51.9 us -> 1.34 us  [local_step(): mean_loss = jnp.sum(loss) / gb[2, :1]]
    psum x2 -> x0, blocking collectives: 46.7 us -> none  [the longest x1 24.3 us: local_step(): lax.psum(jnp.stack([jnp.sum(shifted_exp, axis=1), picked_part]), 'tp')]
    reduce_scatter x1 -> x0, waiting for transfers between devices: 44.7 us -> none  [local_step(): dx_local = lax.psum_scatter(dx_part, 'tp', scatter_dimension=0, tiled=True)]
    all_gather x1 -> x0, waiting for transfers between devices: 43.6 us -> none  [local_step(): lax.all_gather(normed.astype(jnp.bfloat16), 'tp', axis=0, tiled=True)]
    pmax x1 -> x0, blocking collectives: 22.3 us -> none  [local_step(): row_max = lax.pmax(local_max, 'tp')]
  transfers between devices with their start and end apart: 2 -> 0, of which waited for: 2 -> 0; matrix products, arithmetic and copies ran while one was open for 16% -> 0% of each run, Pallas kernels for 0% -> 0%
where the time goes in v1:
time: 359 us; the launch traced here: 358 us
  Pallas kernels  342 us (95%)
  local copies, waits for them, and re-layouts  10.9 us (3%)
    pallas_call x1, Pallas kernels, fused(): pl.pallas_call(fused_kernel, out_shape=(sds((NB, nc * full, vb), bf16), s...  265 us
    pallas_call x1, Pallas kernels, embed_grad(): pl.pallas_call(grad_kernel, grid=(nb, 2), out_shape=jax.ShapeDtypeStruct(...  77.2 us

profile of v1, /device:TPU:0, one launch (start us, length us, event | category | flops | bytes accessed | tf_op | source)
XLA Modules:
  0.0 358.3 jit_solution(16847677576391433997)
XLA Ops:
  0.7 0.1 broadcast_in_dim.27
  0.8 0.1 broadcast_in_dim.28
  0.9 0.8 stack.9
  1.6 0.8 stack.10
  2.4 1.3 reshape.59.gam_ref
  3.7 1.3 reshape.60.bet_ref
  5.0 0.1 broadcast_in_dim.31
  5.0 0.6 broadcast_select_fusion.tm_ref
  5.7 1.4 reshape.62.valid_ref
  7.0 265.1 %shard_map.118 = (bf16[5,4096,1280]{2,1,0:T(8,128)(2,1)}, bf16[8,512,1280]{2,1,0:T(8,128)(2,1)}, bf16[512,1280]{1,0:T(8,128)(2,1)}, f32[8,4,128]{2,1,0:T(4,128)}, f32[8,1280]{1,0:T(8,128)}) custom-call(bf16[512,1280]{1,0:T(8,128)(2,1)} %hid_ref.1, f32[1,1280]{1,0:T(1,128)} %reshape.59.gam_ref, f32[1,1280]{1,0:T(1,128)} %reshape.60.bet_ref, ...), custom_call_target="tpu_custom_call" | custom-call | flops 134217728000 | bytes 100000000 | tf_op jit(solution)/shard_map/pallas_call | solution.py:408
  272.1 1.2 slice.9
  273.3 1.3 reduce_sum.9
  276.0 1.5 slice_reduce_fusion
  277.4 0.8 reshape.63
  278.3 0.7 reshape.64
  278.9 0.0 copy-start
  278.9 77.2 %shard_map.119 = f32[6400,1280]{1,0:T(8,128)} custom-call(bf16[5,4096,1280]{2,1,0:T(8,128)(2,1)} %get-tuple-element.14.dz_ref, bf16[4096,1280]{1,0:T(8,128)(2,1)} %bitcast.5), custom_call_target="tpu_custom_call" | custom-call | flops 67108864000 | bytes 100000000 | tf_op jit(solution)/shard_map/pallas_call | solution.py:452
  356.1 0.0 copy-done
  356.1 1.1 copy.14
  (4 shorter events, 0.0 us)
Async XLA Ops:
  278.9 77.2 %copy-start = (bf16[512,1280]{1,0:T(8,128)(2,1)S(1)}, bf16[512,1280]{1,0:T(8,128)(2,1)}, u32[]{:S(2)}) copy-start(bf16[512,1280]{1,0:T(8,128)(2,1)} %get-tuple-element.26) | copy-start | bytes 3932164

commit v2 on v1

--- a/solution.py
+++ b/solution.py
@@ -10,6 +10,7 @@
 LN_EPS = 1e-5
 LANES = 128
 NB = 5
+AHEAD = 3
 LAG = NB + 1
 LOW = float(jnp.finfo(jnp.float32).min)
 MESH = pl.DeviceIdType.MESH
@@ -21,9 +22,9 @@
 
 
 def fused_kernel(
-    hid_ref, gam_ref, bet_ref, emb_hbm, valid_ref, tm_ref,
-    dz_hbm, xall_hbm, dh_ref, loss_ref, gb_ref,
-    xv, ev, ring, acc, dzb, bias, m_sc, s_sc, p_sc, t1_sc, t2_sc, lse_sc, w_sc,
+    hid_ref, gam_in, bet_in, valid_in, tgt_in, mask_in, emb_hbm,
+    dz_hbm, xall_hbm, dh_ref, tl_ref, gb_ref,
+    par_ref, tm_src, loss_ref, xv, ev, ring, acc, dzb, bias, m_sc, s_sc, p_sc, t1_sc, t2_sc, lse_sc, w_sc,
     tm_all, st_send, st_recv, r0, r1, r2, gb_send, gb_recv,
     e_sem, ag_send, ag_recv, fw_send, tm_send, tm_recv, st_ssem, st_rsem,
     s0, q0, s1, q1, s2, q2, free0, free1, free2, gb_ssem, gb_rsem, dz_sem, x_sem,
@@ -66,10 +67,20 @@
         pl.semaphore_signal(barrier, inc=1, device_id={"tp": lax.rem(me + k, 8)}, device_id_type=MESH)
     pl.semaphore_wait(barrier, 7)
 
-    tm_all[me] = tm_ref[...]
+    lane1 = lax.broadcasted_iota(jnp.int32, (1, LANES), 1)
+    mine = (lane1 >= LANES // 2) == (xc == 1)
+    for i, ref in enumerate((tgt_in, mask_in)):
+        for c in range(nc):
+            row = ref[c // 2:c // 2 + 1].astype(jnp.float32)
+            row = jnp.where(xc == c % 2, row, pltpu.roll(row, LANES // 2, 1))
+            tm_src[i, c:c + 1] = jnp.where(mine, row, 0.0)
+    for r in range(dim // LANES):
+        par_ref[0:1, pl.ds(r * LANES, LANES)] = gam_in[r:r + 1]
+        par_ref[1:2, pl.ds(r * LANES, LANES)] = bet_in[r:r + 1]
+    tm_all[me] = tm_src[...]
 
     def tm_copy(k):
-        return rcopy(tm_ref, tm_all.at[me], tm_send.at[k], tm_recv.at[k], lax.rem(me + k, 8))
+        return rcopy(tm_src, tm_all.at[me], tm_send.at[k], tm_recv.at[k], lax.rem(me + k, 8))
 
     for k in range(1, 8):
         tm_copy(k).start()
@@ -88,21 +99,24 @@
         r = xv.at[c, rows(remote[k][1])]
         return rcopy(r, r, fw_send.at[c, k], ag_recv.at[c, 4 + k], sib)
 
+    def ag_start(c):
+        for k in (2, 0, 1, 3):
+            ag_copy(c, k).start()
+
     def ln_body(c, _):
         xhat, _r = ln(c)
-        xv[c, rows(my_slot), :] = (xhat * gam_ref[...] + bet_ref[...]).astype(jnp.bfloat16)
-
-        @pl.when(c >= 1)
+        xv[c, rows(my_slot), :] = (xhat * par_ref[0:1] + par_ref[1:2]).astype(jnp.bfloat16)
+
+        @pl.when((c >= 1) & (c <= AHEAD))
         def _():
-            for k in (2, 0, 1, 3):
-                ag_copy(c - 1, k).start()
+            ag_start(c - 1)
         return 0
 
     lax.fori_loop(0, nc, ln_body, 0)
-    for k in (2, 0, 1, 3):
-        ag_copy(nc - 1, k).start()
-
-    bias[...] = jnp.where(valid_ref[...] > 0, 0.0, -jnp.inf)
+
+    for r in range(NB * vb // LANES):
+        col = pl.ds(r % (vb // LANES) * LANES, LANES)
+        bias[r // (vb // LANES), :, col] = jnp.where(valid_in[r:r + 1] > 0, 0.0, -jnp.inf)
     gb_send[...] = jnp.zeros_like(gb_send)
 
     def recv_remote(c):
@@ -165,9 +179,10 @@
                 p = p + st_recv[c, d, q, 2:3]
             lse = mx + jnp.log(s)
             loss_ref[c, pl.ds(q, 1), :] = (lse - p) * mk[q]
+            w = mk[q] * inv_n
             r = pl.ds(q * LANES, LANES)
-            lse_sc[r] = _spread(lse)
-            w_sc[r] = _spread(mk[q] * inv_n)
+            lse_sc[r] = _spread(lse - jnp.log(w))
+            w_sc[r] = _spread(w)
             t2_sc[r] = _spread(tg[q]).astype(jnp.int32)
 
     def begin_chunk(c):
@@ -177,6 +192,10 @@
             else:
                 fw_copy(c, k - 4).wait_recv()
         pltpu.make_async_copy(xv.at[c], xall_hbm.at[c], x_sem.at[c]).start()
+        for n in range(2):
+            @pl.when((c >= 1) & (AHEAD + 2 * (c - 1) + n < nc))
+            def _(n=n):
+                ag_start(AHEAD + 2 * (c - 1) + n)
         m_sc[...] = jnp.full(m_sc.shape, LOW, jnp.float32)
         s_sc[...] = jnp.zeros_like(s_sc)
         p_sc[...] = jnp.zeros_like(p_sc)
@@ -249,7 +268,7 @@
         xhat, rstd = ln(c)
         gb_send[0:1] += jnp.sum(dy * xhat, axis=0, keepdims=True)
         gb_send[1:2] += jnp.sum(dy, axis=0, keepdims=True)
-        dxh = dy * gam_ref[...]
+        dxh = dy * par_ref[0:1]
         m1 = jnp.mean(dxh, axis=1, keepdims=True)
         m2 = jnp.mean(dxh * xhat, axis=1, keepdims=True)
         dh_ref[pl.ds(pl.multiple_of(c * own, own), own), :] = (rstd * (dxh - m1 - xhat * m2)).astype(jnp.bfloat16)
@@ -264,36 +283,46 @@
     def compute(t, do1, do2):
         slot = lax.rem(t, LAG)
         a2 = lax.rem(t, 2)
+        cut = (vb // LANES + 1) // 4 * 2 * LANES if vb % 256 else (vb // 256 + 1) // 2 * 256
+        pieces = ((0, cut), (cut, vb))
+        j1 = lax.rem(t, NB)
+        zs = []
         if do2:
             t2 = t - LAG
             j2 = lax.rem(t2, NB)
-            tr = t2_sc[...] - (base + j2 * vb)
-            for k in range(vb // LANES):
-                col = k * LANES
-                p = jnp.exp(ring[slot, :, pl.ds(col, LANES)] - lse_sc[...])
-                p = jnp.where(tr == lane + col, p - 1.0, p) * w_sc[...]
-                dzb[a2, :, pl.ds(col, LANES)] = p.astype(jnp.bfloat16)
+            a = lax.rem(t2 // NB, 2)
+            tr2 = t2_sc[...] - (base + j2 * vb)
+        for lo, hi in pieces:
+            if do2:
+                for col in range(lo, hi, LANES):
+                    p = jnp.exp(ring[slot, :, pl.ds(col, LANES)] - lse_sc[...])
+                    p = p - jnp.where(tr2 == lane + col, w_sc[...], 0.0)
+                    dzb[a2, :, pl.ds(col, LANES)] = p.astype(jnp.bfloat16)
+            if do1:
+                zs.append(lax.dot_general(xv[t // NB], ev[j1, pl.ds(lo, hi - lo), :], NT, preferred_element_type=jnp.float32))
         if do1:
-            j1 = lax.rem(t, NB)
-            tr = t1_sc[...] - (base + j1 * vb)
-            z = lax.dot_general(xv[t // NB], ev[j1], NT, preferred_element_type=jnp.float32) + bias[j1]
-            ring[slot] = z
-            zs = [z[:, k * LANES:(k + 1) * LANES] for k in range(vb // LANES)]
-            m0 = m_sc[...]
-            m = m0
-            for q in zs:
-                m = jnp.maximum(m, q)
-            s = s_sc[...] * jnp.exp(m0 - m)
-            pk = p_sc[...]
-            for k, q in enumerate(zs):
-                s = s + jnp.exp(q - m)
-                pk = pk + jnp.where(tr == lane + k * LANES, q, 0.0)
-            m_sc[...] = m
-            s_sc[...] = s
-            p_sc[...] = pk
-        if do2:
-            a = lax.rem(t2 // NB, 2)
-            acc[a] = acc[a] + jnp.dot(dzb[a2], ev[j2], preferred_element_type=jnp.float32)
+            tr1 = t1_sc[...] - (base + j1 * vb)
+        for n, (lo, hi) in enumerate(pieces):
+            w = pl.ds(lo, hi - lo)
+            if do2:
+                acc[a, :, pl.ds(lo * dim // vb, (hi - lo) * dim // vb)] += jnp.dot(
+                    dzb[a2], ev[j2, :, pl.ds(lo * dim // vb, (hi - lo) * dim // vb)], preferred_element_type=jnp.float32)
+            if do1:
+                z = zs[n] + bias[j1, :, w]
+                ring[slot, :, w] = z
+                cols = [z[:, k * LANES:(k + 1) * LANES] for k in range((hi - lo) // LANES)]
+                m0 = m_sc[...]
+                m = m0
+                for q in cols:
+                    m = jnp.maximum(m, q)
+                s = s_sc[...] * jnp.exp(m0 - m)
+                pk = p_sc[...]
+                for k, q in enumerate(cols):
+                    s = s + jnp.exp(q - m)
+                    pk = pk + jnp.where(tr1 == lane + (lo + k * LANES), q, 0.0)
+                m_sc[...] = m
+                s_sc[...] = s
+                p_sc[...] = pk
 
     def step(t, do1, do2):
         ph = lax.rem(t, NB)
@@ -388,10 +417,20 @@
     for d in range(1, 8):
         tot = tot + gb_recv[d]
     gb_ref[...] = tot
-    gb_ref[2:3] = jnp.broadcast_to(count, (1, dim))
-
-
-def fused(hidden, gamma, beta, embed, valid, tm):
+    mean = jnp.zeros((4, LANES), jnp.float32)
+    for c in range(nc):
+        mean = mean + loss_ref[c]
+    mean = jnp.sum(jnp.sum(mean, axis=1, keepdims=True), axis=0, keepdims=True) / count
+    gb_ref[2:3] = jnp.broadcast_to(mean, (1, dim))
+    for r in range(nc // 2):
+        halves = []
+        for n in range(2):
+            row = loss_ref[2 * r + n, pl.ds(my_slot // 2, 1), :]
+            halves.append(jnp.where(xc == n, row, pltpu.roll(row, LANES // 2, 1)))
+        tl_ref[r:r + 1] = jnp.where(lane1 < LANES // 2, halves[0], halves[1])
+
+
+def fused(hidden, gamma, beta, valid, tgt, mask, embed):
     tok, dim = hidden.shape
     nc = 8
     own = tok // nc
@@ -411,12 +450,15 @@
             sds((NB, nc * full, vb), bf16),
             sds((nc, full, dim), bf16),
             sds((tok, dim), bf16),
-            sds((nc, 4, LANES), f32),
+            sds((nc // 2, LANES), f32),
             sds((8, dim), f32),
         ),
-        in_specs=[vmem, vmem, vmem, hbm, vmem, vmem],
+        in_specs=[vmem] * 6 + [hbm],
         out_specs=(hbm, hbm, vmem, vmem, vmem),
         scratch_shapes=[
+            pltpu.VMEM((8, dim), f32),
+            pltpu.VMEM((2, nc, LANES), f32),
+            pltpu.VMEM((nc, 4, LANES), f32),
             pltpu.VMEM((nc, full, dim), bf16),
             pltpu.VMEM((NB, vb, dim), bf16),
             pltpu.VMEM((LAG, full, vb), f32),
@@ -438,29 +480,50 @@
         ],
         compiler_params=pltpu.CompilerParams(collective_id=0, has_side_effects=True, vmem_limit_bytes=67043328),
         cost_estimate=pl.CostEstimate(flops=flops, bytes_accessed=100_000_000, transcendentals=0),
-    )(hidden, gamma, beta, embed.reshape(NB, vb, dim), valid, tm)
-
-
-def grad_kernel(dz_ref, x_ref, o_ref):
+    )(hidden, gamma, beta, valid, tgt, mask, embed.reshape(NB, vb, dim))
+
+
+def grad_kernel(dz_ref, x_ref, dh_in, tl_in, gb_in, o_ref, dh_ref, tl_ref, dg_ref, db_ref, ml_ref):
+    @pl.when((pl.program_id(0) == 0) & (pl.program_id(1) == 0))
+    def _():
+        dh_ref[...] = dh_in[...]
+        tl_ref[...] = tl_in[...]
+        for r in range(dg_ref.shape[0]):
+            dg_ref[r:r + 1] = gb_in[0:1, r * LANES:(r + 1) * LANES]
+            db_ref[r:r + 1] = gb_in[1:2, r * LANES:(r + 1) * LANES]
+        ml_ref[...] = gb_in[2:3, 0:1]
+
     o_ref[...] = lax.dot_general(dz_ref[...], x_ref[...], (((0,), (0,)), ((), ())), preferred_element_type=jnp.float32)
 
 
-def embed_grad(dz, x):
+def embed_grad(dz, x, d_hidden, tl, gb):
     nb, toks, vb = dz.shape
     dim = x.shape[1]
     mb = vb // 2
+    f32 = jnp.float32
+    sds = jax.ShapeDtypeStruct
+
+    def whole(shape):
+        return pl.BlockSpec(shape, lambda i, k: (0, 0), pipeline_mode=pl.Buffered(1))
+
     return pl.pallas_call(
         grad_kernel,
         grid=(nb, 2),
-        out_shape=jax.ShapeDtypeStruct((nb * vb, dim), jnp.float32),
+        out_shape=(
+            sds((nb * vb, dim), f32), sds(d_hidden.shape, d_hidden.dtype), sds(tl.shape, f32),
+            sds((dim // LANES, LANES), f32), sds((dim // LANES, LANES), f32), sds((1, 1), f32),
+        ),
         in_specs=[
             pl.BlockSpec((None, toks, mb), lambda i, k: (i, 0, k)),
-            pl.BlockSpec((toks, dim), lambda i, k: (0, 0), pipeline_mode=pl.Buffered(1)),
+            whole((toks, dim)), whole(d_hidden.shape), whole(tl.shape), whole(gb.shape),
         ],
-        out_specs=pl.BlockSpec((mb, dim), lambda i, k: (i * 2 + k, 0)),
+        out_specs=(
+            pl.BlockSpec((mb, dim), lambda i, k: (i * 2 + k, 0)),
+            whole(d_hidden.shape), whole(tl.shape), whole((dim // LANES, LANES)), whole((dim // LANES, LANES)), whole((1, 1)),
+        ),
         compiler_params=pltpu.CompilerParams(vmem_limit_bytes=62 * 1024 * 1024),
         cost_estimate=pl.CostEstimate(flops=2 * toks * nb * vb * dim, bytes_accessed=100_000_000, transcendentals=0),
-    )(dz, x)
+    )(dz, x, d_hidden, tl, gb)
 
 
 def solution(mesh):
@@ -469,18 +532,12 @@
 
     def local_step(hidden, gamma, beta, embed, valid, tgt, mask):
         tok, dim = hidden.shape
-        own = tok // 8
-        me = lax.axis_index("tp")
-        core, xc, yc = me % 2, (me // 2) % 2, me // 4
-        slot = core * 4 + yc * 2 + xc
-        tm = jnp.stack([tgt, mask]).astype(jnp.float32).reshape(2, 8, 1, own)
-        tm = jnp.where((jnp.arange(2) == xc)[None, None, :, None], tm, 0.0).reshape(2, 8, 2 * own)
-        dz, x_all, d_hidden, loss, gb = fused(
-            hidden, gamma.reshape(1, dim), beta.reshape(1, dim), embed, valid.reshape(NB, 1, -1), tm)
-        d_embed = embed_grad(dz, x_all.reshape(-1, dim))
-        tok_loss = lax.dynamic_index_in_dim(loss.reshape(8, 8, own), slot, axis=1, keepdims=False).reshape(-1)
-        mean_loss = jnp.sum(loss) / gb[2, :1]
-        return tok_loss, mean_loss, d_hidden, d_embed, gb[0], gb[1]
+        def rows(v):
+            return v.reshape(-1, LANES)
+
+        dz, x_all, d_hidden, tl, gb = fused(hidden, rows(gamma), rows(beta), rows(valid), rows(tgt), rows(mask), embed)
+        d_embed, d_hidden, tl, dg, db, ml = embed_grad(dz, x_all.reshape(-1, dim), d_hidden, tl, gb)
+        return tl.reshape(-1), ml.reshape(1), d_hidden, d_embed, dg.reshape(-1), db.reshape(-1)
 
     return jax.shard_map(
         local_step,

time: 359 us -> 319 us (0.89)
  Pallas kernels: 342 us -> 319 us
  local copies, waits for them, and re-layouts: 10.9 us -> 0 us
    pallas_call x1, Pallas kernels: 265 us -> 241 us  [fused(): pl.pallas_call(fused_kernel, out_shape=(sds((NB, nc * full, vb), bf16), s...]
    reshape x5 -> x0, local copies, waits for them, and re-layouts: 5.42 us -> none  [the longest x1 1.38 us: local_step(): valid.reshape(NB, 1, -1)]
where the time goes in v2:
time: 319 us
  Pallas kernels  319 us (100%)
    pallas_call x1, Pallas kernels, fused(): pl.pallas_call(fused_kernel, out_shape=(sds((NB, nc * full, vb), bf16), s...  241 us
    pallas_call x1, Pallas kernels, embed_grad(): pl.pallas_call(grad_kernel, grid=(nb, 2), out_shape=(sds((nb * vb, dim),...  78 us

profile of v2, /device:TPU:0, one launch (start us, length us, event | category | flops | bytes accessed | tf_op | source)
XLA Modules:
  0.0 319.4 jit_solution(5146122292998206766)
XLA Ops:
  0.6 240.7 %shard_map.118 = (bf16[5,4096,1280]{2,1,0:T(8,128)(2,1)}, bf16[8,512,1280]{2,1,0:T(8,128)(2,1)}, bf16[512,1280]{1,0:T(8,128)(2,1)}, f32[4,128]{1,0:T(4,128)}, f32[8,1280]{1,0:T(8,128)}) custom-call(bf16[512,1280]{1,0:T(8,128)(2,1)} %hid_ref.1, f32[10,128]{1,0:T(8,128)} %bitcast.13, f32[10,128]{1,0:T(8,128)} %bitcast.14, s32[50,128]{1,0:T(8,128)} %bitcast.12, ...), custom_call_target="tpu_custom_call" | custom-call | flops 134217728000 | bytes 100000000 | tf_op jit(solution)/shard_map/pallas_call | solution.py:447
  241.3 78.0 %shard_map.119 = (f32[6400,1280]{1,0:T(8,128)}, bf16[512,1280]{1,0:T(8,128)(2,1)}, f32[4,128]{1,0:T(4,128)}, f32[10,128]{1,0:T(8,128)}, f32[10,128]{1,0:T(8,128)}, /*index=5*/f32[1,1]{1,0:T(1,128)}) custom-call(bf16[5,4096,1280]{2,1,0:T(8,128)(2,1)} %get-tuple-element.17.dz_ref, bf16[4096,1280]{1,0:T(8,128)(2,1)} %bitcast.17, ...), custom_call_target="tpu_custom_call" | custom-call | flops 67108864000 | bytes 100000000 | tf_op jit(solution)/shard_map/pallas_call | solution.py:509

commit v3 on v2

--- a/solution.py
+++ b/solution.py
@@ -23,11 +23,11 @@
 
 def fused_kernel(
     hid_ref, gam_in, bet_in, valid_in, tgt_in, mask_in, emb_hbm,
-    dz_hbm, xall_hbm, dh_ref, tl_ref, gb_ref,
+    dz_hbm, xall_hbm, de_hbm, dh_ref, tl_ref, gb_ref,
     par_ref, tm_src, loss_ref, xv, ev, ring, acc, dzb, bias, m_sc, s_sc, p_sc, t1_sc, t2_sc, lse_sc, w_sc,
     tm_all, st_send, st_recv, r0, r1, r2, gb_send, gb_recv,
     e_sem, ag_send, ag_recv, fw_send, tm_send, tm_recv, st_ssem, st_rsem,
-    s0, q0, s1, q1, s2, q2, free0, free1, free2, gb_ssem, gb_rsem, dz_sem, x_sem,
+    s0, q0, s1, q1, s2, q2, free0, free1, free2, gb_ssem, gb_rsem, dz_sem, x_sem, fz_sem, de_sem,
 ):
     nc, tok, dim = xv.shape
     vb = ev.shape[1]
@@ -65,7 +65,6 @@
     barrier = pltpu.get_barrier_semaphore()
     for k in range(1, 8):
         pl.semaphore_signal(barrier, inc=1, device_id={"tp": lax.rem(me + k, 8)}, device_id_type=MESH)
-    pl.semaphore_wait(barrier, 7)
 
     lane1 = lax.broadcasted_iota(jnp.int32, (1, LANES), 1)
     mine = (lane1 >= LANES // 2) == (xc == 1)
@@ -82,9 +81,6 @@
     def tm_copy(k):
         return rcopy(tm_src, tm_all.at[me], tm_send.at[k], tm_recv.at[k], lax.rem(me + k, 8))
 
-    for k in range(1, 8):
-        tm_copy(k).start()
-
     def ln(c):
         h = hid_ref[pl.ds(pl.multiple_of(c * own, own), own), :].astype(jnp.float32)
         cen = h - jnp.mean(h, axis=1, keepdims=True)
@@ -103,17 +99,26 @@
         for k in (2, 0, 1, 3):
             ag_copy(c, k).start()
 
+    def ln_store(c):
+        xhat, _ = ln(c)
+        xv[c, rows(my_slot), :] = (xhat * par_ref[0:1] + par_ref[1:2]).astype(jnp.bfloat16)
+
+    for c in range(2):
+        ln_store(c)
+    pl.semaphore_wait(barrier, 7)
+    ag_start(0)
+    for k in range(1, 8):
+        tm_copy(k).start()
+
     def ln_body(c, _):
-        xhat, _r = ln(c)
-        xv[c, rows(my_slot), :] = (xhat * par_ref[0:1] + par_ref[1:2]).astype(jnp.bfloat16)
-
-        @pl.when((c >= 1) & (c <= AHEAD))
+        ln_store(c)
+
+        @pl.when(c <= AHEAD)
         def _():
             ag_start(c - 1)
         return 0
 
-    lax.fori_loop(0, nc, ln_body, 0)
-
+    lax.fori_loop(2, nc, ln_body, 0)
     for r in range(NB * vb // LANES):
         col = pl.ds(r % (vb // LANES) * LANES, LANES)
         bias[r // (vb // LANES), :, col] = jnp.where(valid_in[r:r + 1] > 0, 0.0, -jnp.inf)
@@ -150,15 +155,13 @@
         return rcopy(st_send.at[c], st_recv.at[c, me], st_ssem.at[c, k], st_rsem.at[c, k], lax.rem(me + k, 8))
 
     def send_stats(c):
-        li = lax.broadcasted_iota(jnp.int32, (LANES, LANES), 1)
         for q in range(4):
             r = pl.ds(q * LANES, LANES)
-            m = m_sc[r]
-            mx = jnp.max(m, axis=1, keepdims=True)
-            s = jnp.sum(s_sc[r] * jnp.exp(m - mx), axis=1, keepdims=True)
-            p = jnp.sum(p_sc[r], axis=1, keepdims=True)
-            v = jnp.where(li == 0, mx, jnp.where(li == 1, s, p))
-            st_send[c, q] = v.T[:8]
+            m = m_sc[r].T
+            mx = jnp.max(m, axis=0, keepdims=True)
+            st_send[c, q, 0:1] = mx
+            st_send[c, q, 1:2] = jnp.sum(s_sc[r].T * jnp.exp(m - mx), axis=0, keepdims=True)
+            st_send[c, q, 2:3] = jnp.sum(p_sc[r].T, axis=0, keepdims=True)
         st_recv[c, me] = st_send[c]
         for k in range(1, 8):
             st_copy(c, k).start()
@@ -378,16 +381,55 @@
             return 0
         lax.fori_loop(lo, hi, body, 0)
 
+    spans = [(n, lo, min(tok, vb - lo)) for n, lo in enumerate(range(0, vb, tok))]
+
+    def fz_copy(c):
+        a = lax.rem(c, 2)
+        return pltpu.make_async_copy(dz_hbm.at[0, pl.ds(pl.multiple_of(c * tok, tok), tok)], dzb.at[a], fz_sem.at[a])
+
+    def de_copy(n, lo, size):
+        return pltpu.make_async_copy(ring.at[n, pl.ds(0, size)], de_hbm.at[pl.ds(lo, size)], de_sem.at[n])
+
+    last = nc - 1
+
+    def fill(f, _):
+        @pl.when(f == 0)
+        def _():
+            stage0(last)
+            for n, lo, size in spans:
+                ring[n, :size] = jnp.zeros((size, dim), jnp.float32)
+
+        @pl.when(f == 1)
+        def _():
+            stage3(last - 1)
+
+        @pl.when(f == 2)
+        def _():
+            stage1(last)
+
+        @pl.when(f == nc - 2)
+        def _():
+            stage2(last)
+        fz_copy(f).wait()
+        a = lax.rem(f, 2)
+        for n, lo, size in spans:
+            ring[n, :size] += lax.dot_general(dzb[a, :, pl.ds(lo, size)], xv[f], (((0,), (0,)), ((), ())), preferred_element_type=jnp.float32)
+
+        @pl.when(f + 2 < nc)
+        def _():
+            fz_copy(f + 2).start()
+        return 0
+
     total = NB * nc
     loop(0, LAG, True, False)
     loop(LAG, total, True, True)
     loop(total, total + LAG, False, True)
-
-    last = nc - 1
-    stage0(last)
-    stage3(last - 1)
-    stage1(last)
-    stage2(last)
+    for c in range(2):
+        dz_copy(total + LAG - 2 + c).wait()
+        fz_copy(lax.rem(total + LAG + c, 2)).start()
+    lax.fori_loop(0, nc, fill, 0)
+    for span in spans:
+        de_copy(*span).start()
     stage3(last)
 
     def gb_copy(k):
@@ -396,8 +438,8 @@
     for k in range(1, 8):
         gb_copy(k).start()
     gb_recv[me] = gb_send[...]
-    for t in (total + LAG - 2, total + LAG - 1):
-        dz_copy(t).wait()
+    for span in spans:
+        de_copy(*span).wait()
 
     def drain(c, _):
         for k in range(4):
@@ -449,12 +491,13 @@
         out_shape=(
             sds((NB, nc * full, vb), bf16),
             sds((nc, full, dim), bf16),
+            sds((vb, dim), f32),
             sds((tok, dim), bf16),
             sds((nc // 2, LANES), f32),
             sds((8, dim), f32),
         ),
         in_specs=[vmem] * 6 + [hbm],
-        out_specs=(hbm, hbm, vmem, vmem, vmem),
+        out_specs=(hbm, hbm, hbm, vmem, vmem, vmem),
         scratch_shapes=[
             pltpu.VMEM((8, dim), f32),
             pltpu.VMEM((2, nc, LANES), f32),
@@ -476,54 +519,109 @@
             pltpu.VMEM((8, 8, dim), f32),
             dma((NB,)), dma((nc, 4)), dma((nc, 7)), dma((nc, 3)), dma((8,)), dma((8,)), dma((nc, 8)), dma((nc, 8)),
             dma((2,)), dma((2,)), dma((2, 2)), dma((2, 2)), dma((2,)), dma((2,)),
-            reg, reg, reg, dma((8,)), dma((8,)), dma((2,)), dma((nc,)),
+            reg, reg, reg, dma((8,)), dma((8,)), dma((2,)), dma((nc,)), dma((2,)), dma((4,)),
         ],
         compiler_params=pltpu.CompilerParams(collective_id=0, has_side_effects=True, vmem_limit_bytes=67043328),
         cost_estimate=pl.CostEstimate(flops=flops, bytes_accessed=100_000_000, transcendentals=0),
     )(hidden, gamma, beta, valid, tgt, mask, embed.reshape(NB, vb, dim))
 
 
-def grad_kernel(dz_ref, x_ref, dh_in, tl_in, gb_in, o_ref, dh_ref, tl_ref, dg_ref, db_ref, ml_ref):
-    @pl.when((pl.program_id(0) == 0) & (pl.program_id(1) == 0))
+def grad_kernel(dz_ref, x_hbm, de_in, dh_in, tl_in, gb_in, o_hbm, dh_ref, tl_ref, dg_ref, db_ref, ml_ref, xbuf, obuf, ebuf, x_sem, o_sem, e_sem):
+    s = pl.program_id(0)
+    steps = pl.num_programs(0)
+    parts, depth, _ = xbuf.shape
+    mb = obuf.shape[1]
+    edge = ebuf.shape[0]
+    slot = lax.rem(s, 2)
+    tn = (((0,), (0,)), ((), ()))
+
+    def x_copy(n):
+        return pltpu.make_async_copy(x_hbm.at[n], xbuf.at[n], x_sem.at[n])
+
+    def out_copy(t):
+        a = lax.rem(t, 2)
+        return pltpu.make_async_copy(obuf.at[a], o_hbm.at[pl.ds(pl.multiple_of(edge + t * mb, mb), mb)], o_sem.at[a])
+
+    e_in = pltpu.make_async_copy(de_in, ebuf, e_sem.at[0])
+    e_out = pltpu.make_async_copy(ebuf, o_hbm.at[pl.ds(0, edge)], e_sem.at[1])
+
+    @pl.when(s == 0)
     def _():
+        for n in range(parts):
+            x_copy(n).start()
         dh_ref[...] = dh_in[...]
         tl_ref[...] = tl_in[...]
         for r in range(dg_ref.shape[0]):
             dg_ref[r:r + 1] = gb_in[0:1, r * LANES:(r + 1) * LANES]
             db_ref[r:r + 1] = gb_in[1:2, r * LANES:(r + 1) * LANES]
         ml_ref[...] = gb_in[2:3, 0:1]
-
-    o_ref[...] = lax.dot_general(dz_ref[...], x_ref[...], (((0,), (0,)), ((), ())), preferred_element_type=jnp.float32)
-
-
-def embed_grad(dz, x, d_hidden, tl, gb):
+        for n in range(parts):
+            x_copy(n).wait()
+            part = lax.dot_general(dz_ref[pl.ds(n * depth, depth)], xbuf[n], tn, preferred_element_type=jnp.float32)
+            if n == 0:
+                obuf[0] = part
+            else:
+                obuf[0] += part
+        e_in.start()
+
+    @pl.when(s > 0)
+    def _():
+        @pl.when(s >= 2)
+        def _():
+            out_copy(s - 2).wait()
+
+        @pl.when(s == 2)
+        def _():
+            e_in.wait()
+            e_out.start()
+        obuf[slot] = lax.dot_general(dz_ref[...], xbuf[...].reshape(parts * depth, -1), tn, preferred_element_type=jnp.float32)
+
+    out_copy(s).start()
+
+    @pl.when(s == steps - 1)
+    def _():
+        e_out.wait()
+        out_copy(s - 1).wait()
+        out_copy(s).wait()
+
+
+def embed_grad(dz, x, de, d_hidden, tl, gb):
     nb, toks, vb = dz.shape
-    dim = x.shape[1]
+    dim = x.shape[-1]
     mb = vb // 2
+    parts = 4
     f32 = jnp.float32
     sds = jax.ShapeDtypeStruct
+    hbm = pl.BlockSpec(memory_space=pl.ANY)
+    dma = pltpu.SemaphoreType.DMA
 
     def whole(shape):
-        return pl.BlockSpec(shape, lambda i, k: (0, 0), pipeline_mode=pl.Buffered(1))
+        return pl.BlockSpec(shape, lambda s: (0, 0), pipeline_mode=pl.Buffered(1))
 
     return pl.pallas_call(
         grad_kernel,
-        grid=(nb, 2),
+        grid=((nb - 1) * 2,),
         out_shape=(
             sds((nb * vb, dim), f32), sds(d_hidden.shape, d_hidden.dtype), sds(tl.shape, f32),
             sds((dim // LANES, LANES), f32), sds((dim // LANES, LANES), f32), sds((1, 1), f32),
         ),
         in_specs=[
-            pl.BlockSpec((None, toks, mb), lambda i, k: (i, 0, k)),
-            whole((toks, dim)), whole(d_hidden.shape), whole(tl.shape), whole(gb.shape),
+            pl.BlockSpec((None, toks, mb), lambda s: (1 + s // 2, 0, s % 2)),
+            hbm, hbm, whole(d_hidden.shape), whole(tl.shape), whole(gb.shape),
         ],
         out_specs=(
-            pl.BlockSpec((mb, dim), lambda i, k: (i * 2 + k, 0)),
+            hbm,
             whole(d_hidden.shape), whole(tl.shape), whole((dim // LANES, LANES)), whole((dim // LANES, LANES)), whole((1, 1)),
         ),
+        scratch_shapes=[
+            pltpu.VMEM((parts, toks // parts, dim), x.dtype),
+            pltpu.VMEM((2, mb, dim), f32),
+            pltpu.VMEM((vb, dim), f32),
+            dma((parts,)), dma((2,)), dma((2,)),
+        ],
         compiler_params=pltpu.CompilerParams(vmem_limit_bytes=62 * 1024 * 1024),
         cost_estimate=pl.CostEstimate(flops=2 * toks * nb * vb * dim, bytes_accessed=100_000_000, transcendentals=0),
-    )(dz, x, d_hidden, tl, gb)
+    )(dz, x.reshape(parts, toks // parts, dim), de, d_hidden, tl, gb)
 
 
 def solution(mesh):
@@ -535,8 +633,8 @@
         def rows(v):
             return v.reshape(-1, LANES)
 
-        dz, x_all, d_hidden, tl, gb = fused(hidden, rows(gamma), rows(beta), rows(valid), rows(tgt), rows(mask), embed)
-        d_embed, d_hidden, tl, dg, db, ml = embed_grad(dz, x_all.reshape(-1, dim), d_hidden, tl, gb)
+        dz, x_all, de, d_hidden, tl, gb = fused(hidden, rows(gamma), rows(beta), rows(valid), rows(tgt), rows(mask), embed)
+        d_embed, d_hidden, tl, dg, db, ml = embed_grad(dz, x_all.reshape(-1, dim), de, d_hidden, tl, gb)
         return tl.reshape(-1), ml.reshape(1), d_hidden, d_embed, dg.reshape(-1), db.reshape(-1)
 
     return jax.shard_map(

time: 319 us -> 309 us (0.969)
  Pallas kernels: 319 us -> 308 us
    pallas_call x1, Pallas kernels: 78 us -> 67.1 us  [embed_grad(): pl.pallas_call(grad_kernel, grid=((nb - 1) * 2,), out_shape=(sds((nb * vb...]
where the time goes in v3:
time: 309 us
  Pallas kernels  308 us (100%)
    pallas_call x1, Pallas kernels, fused(): pl.pallas_call(fused_kernel, out_shape=(sds((NB, nc * full, vb), bf16), s...  241 us
    pallas_call x1, Pallas kernels, embed_grad(): pl.pallas_call(grad_kernel, grid=((nb - 1) * 2,), out_shape=(sds((nb * vb...  67.1 us

profile of v3, /device:TPU:0, one launch (start us, length us, event | category | flops | bytes accessed | tf_op | source)
XLA Modules:
  0.0 309.0 jit_solution(15942170485968686993)
XLA Ops:
  0.6 241.1 %shard_map.118 = (bf16[5,4096,1280]{2,1,0:T(8,128)(2,1)}, bf16[8,512,1280]{2,1,0:T(8,128)(2,1)}, f32[1280,1280]{1,0:T(8,128)}, bf16[512,1280]{1,0:T(8,128)(2,1)}, f32[4,128]{1,0:T(4,128)}, /*index=5*/f32[8,1280]{1,0:T(8,128)}) custom-call(bf16[512,1280]{1,0:T(8,128)(2,1)} %hid_ref.1, f32[10,128]{1,0:T(8,128)} %bitcast.13, f32[10,128]{1,0:T(8,128)} %bitcast.14, ...), custom_call_target="tpu_custom_call" | custom-call | flops 134217728000 | bytes 100000000 | tf_op jit(solution)/shard_map/pallas_call | solution.py:489
  241.8 67.1 %shard_map.119 = (f32[6400,1280]{1,0:T(8,128)}, bf16[512,1280]{1,0:T(8,128)(2,1)}, f32[4,128]{1,0:T(4,128)}, f32[10,128]{1,0:T(8,128)}, f32[10,128]{1,0:T(8,128)}, /*index=5*/f32[1,1]{1,0:T(1,128)}) custom-call(bf16[5,4096,1280]{2,1,0:T(8,128)(2,1)} %get-tuple-element.18.dz_ref, bf16[4,1024,1280]{2,1,0:T(8,128)(2,1)} %bitcast.17, ...), custom_call_target="tpu_custom_call" | custom-call | flops 67108864000 | bytes 100000000 | tf_op jit(solution)/shard_map/pallas_call | solution.py:601

commit v4 on v3

--- a/solution.py
+++ b/solution.py
@@ -329,41 +329,47 @@
 
     def step(t, do1, do2):
         ph = lax.rem(t, NB)
+        per = t // NB
+
+        @pl.when(ph == 0)
+        def _():
+            if do1:
+                begin_chunk(per)
+            if do2:
+                @pl.when(t >= 15)
+                def _():
+                    stage2(per - 3)
+
+        if do2:
+            @pl.when(ph == 1)
+            def _():
+                @pl.when(t >= 11)
+                def _():
+                    stage0(per - 2)
+                c = per - 1
+                use_stats(c)
+                acc[lax.rem(c, 2)] = jnp.zeros((tok, dim), jnp.float32)
+
+        @pl.when(ph == 2)
+        def _():
+            if do1:
+                @pl.when(per + 1 < nc)
+                def _():
+                    forward(per + 1)
+            if do2:
+                @pl.when(t >= 12)
+                def _():
+                    stage1(per - 2)
+
+                @pl.when(t >= 17)
+                def _():
+                    stage3(per - 3)
+
         if do1:
-            @pl.when(ph == 0)
-            def _():
-                begin_chunk(t // NB)
-
-            @pl.when((ph == 2) & (t // NB + 1 < nc))
-            def _():
-                forward(t // NB + 1)
-
             @pl.when(t < NB)
             def _():
                 pltpu.make_async_copy(emb_hbm.at[ph], ev.at[ph], e_sem.at[ph]).wait()
         if do2:
-            @pl.when((ph == 1) & (t >= 11))
-            def _():
-                stage0((t - 11) // NB)
-
-            @pl.when(ph == 1)
-            def _():
-                c = (t - LAG) // NB
-                use_stats(c)
-                acc[lax.rem(c, 2)] = jnp.zeros((tok, dim), jnp.float32)
-
-            @pl.when((ph == 2) & (t >= 17))
-            def _():
-                stage3((t - 17) // NB)
-
-            @pl.when((ph == 2) & (t >= 12))
-            def _():
-                stage1((t - 12) // NB)
-
-            @pl.when((ph == 0) & (t >= 15))
-            def _():
-                stage2((t - 15) // NB)
-
             @pl.when(t >= LAG + 2)
             def _():
                 dz_copy(t - 2).wait()
@@ -401,11 +407,11 @@
 
         @pl.when(f == 1)
         def _():
+            stage1(last)
+
+        @pl.when(f == 2)
+        def _():
             stage3(last - 1)
-
-        @pl.when(f == 2)
-        def _():
-            stage1(last)
 
         @pl.when(f == nc - 2)
         def _():

time: 309 us -> 306 us (level)
    pallas_call x1, Pallas kernels: 241 us -> 238 us  [fused(): pl.pallas_call(fused_kernel, out_shape=(sds((NB, nc * full, vb), bf16), s...]
where the time goes in v4:
time: 306 us; the launch traced here: 305 us
  Pallas kernels  305 us (100%)
    pallas_call x1, Pallas kernels, fused(): pl.pallas_call(fused_kernel, out_shape=(sds((NB, nc * full, vb), bf16), s...  238 us
    pallas_call x1, Pallas kernels, embed_grad(): pl.pallas_call(grad_kernel, grid=((nb - 1) * 2,), out_shape=(sds((nb * vb...  67.1 us

profile of v4, /device:TPU:0, one launch (start us, length us, event | category | flops | bytes accessed | tf_op | source)
XLA Modules:
  0.0 305.4 jit_solution(13081078371338493119)
XLA Ops:
  0.6 237.6 %shard_map.118 = (bf16[5,4096,1280]{2,1,0:T(8,128)(2,1)}, bf16[8,512,1280]{2,1,0:T(8,128)(2,1)}, f32[1280,1280]{1,0:T(8,128)}, bf16[512,1280]{1,0:T(8,128)(2,1)}, f32[4,128]{1,0:T(4,128)}, /*index=5*/f32[8,1280]{1,0:T(8,128)}) custom-call(bf16[512,1280]{1,0:T(8,128)(2,1)} %hid_ref.1, f32[10,128]{1,0:T(8,128)} %bitcast.13, f32[10,128]{1,0:T(8,128)} %bitcast.14, ...), custom_call_target="tpu_custom_call" | custom-call | flops 134217728000 | bytes 100000000 | tf_op jit(solution)/shard_map/pallas_call | solution.py:495
  238.2 67.1 %shard_map.119 = (f32[6400,1280]{1,0:T(8,128)}, bf16[512,1280]{1,0:T(8,128)(2,1)}, f32[4,128]{1,0:T(4,128)}, f32[10,128]{1,0:T(8,128)}, f32[10,128]{1,0:T(8,128)}, /*index=5*/f32[1,1]{1,0:T(1,128)}) custom-call(bf16[5,4096,1280]{2,1,0:T(8,128)(2,1)} %get-tuple-element.18.dz_ref, bf16[4,1024,1280]{2,1,0:T(8,128)(2,1)} %bitcast.17, ...), custom_call_target="tpu_custom_call" | custom-call | flops 67108864000 | bytes 100000000 | tf_op jit(solution)/shard_map/pallas_call | solution.py:607
